TPU v7x, 128 devices: a whole 4x4x4 slice. The times are simulated.
128 devices in a mesh: slot: 32 (over x, z, y_hi), dp: 4 (over y_lo, core).
Axes of the slice: x: 4, y: 4 (y_hi: 2, y_lo: 2; y = y_hi * 2 + y_lo), z: 4, core: 2. Of those that a mesh axis runs over, the one named last changes fastest.
Arguments:
- tokens: bfloat16 [12, 4096, 1024], P('dp', 'slot'), may hold values from -6 to 6
- slot_keys: bfloat16 [1024, 1024], P(None, 'slot'), may hold values from -1.5 to 1.5
- expert_in: bfloat16 [128, 1024, 4096], P('slot', None, 'dp'), may hold values from -0.5 to 0.5
- expert_out: bfloat16 [128, 4096, 1024], P('slot', 'dp'), may hold values from -0.1875 to 0.1875
Outputs:
- combined: bfloat16 [12, 4096, 1024], P('dp', 'slot')
All inputs are finite; a program needn't handle non-finite values.
Results may differ from a plain program's by a relative error of at most 0.0085.
Values may be sent and summed in bfloat16 or wider, within the bound.
No kernel may reach another device: no remote copies, remote signals or barrier semaphores. Data moves between devices by JAX's collectives and lax.ppermute only.
A program may use at most 128 MiB of HBM per device.

v0:
```python
import jax
import jax.numpy as jnp
from jax import lax
from jax.sharding import Mesh
from jax.sharding import PartitionSpec as P

SLOT = ("slot_0", "slot_1", "slot_2")


def from_everyone(array, axis):
    copies = jnp.broadcast_to(array, (lax.axis_size(axis), *array.shape))
    return lax.all_to_all(copies, axis, split_axis=0, concat_axis=0, tiled=True)


def all_in_one(array, axis):
    leaves = jax.tree.leaves(array)
    turns = sorted(range(len(leaves)), key=lambda k: -leaves[k].size)
    width = (1, *leaves[turns[0]].shape)[-1]
    lines = [
        jnp.pad(leaves[k].reshape(-1), (0, -leaves[k].size % width)).reshape(-1, width)
        for k in turns
    ]
    both, at, found = (from_everyone(jnp.concatenate(lines), axis), 0, {})
    for k, line in zip(turns, lines):
        slab = both[:, at : at + len(line)].reshape(len(both), -1)
        found[k] = slab[:, : leaves[k].size].reshape(-1, *leaves[k].shape)
        at += len(line)
    numbers = iter(range(len(leaves)))
    return jax.tree.map(lambda _: found[next(numbers)], array)


def joined_by_halves(pieces, combine):
    while len(jax.tree.leaves(pieces)[0]) > 1:
        pieces = jax.vmap(combine)(
            *(jax.tree.map(lambda part: part[side::2], pieces) for side in (0, 1))
        )
    return jax.tree.map(lambda part: part[0], pieces)


def merged(array, axis, combine):
    pieces = all_in_one(array, axis)
    return joined_by_halves(pieces, combine)


def summed_rows(total, axes):
    for axis in axes:
        total = lax.psum_scatter(total, axis, scatter_dimension=0, tiled=True)
    return total


def laid_out(pieces, dim):
    pieces = jnp.moveaxis(pieces, 0, dim)
    lengths = pieces.shape
    return pieces.reshape(*lengths[:dim], lengths[dim] * lengths[dim + 1], *lengths[dim + 2 :])


def gathered_copies(array, axis, dim):
    pieces = from_everyone(array, axis)
    return laid_out(pieces, dim)


def cut_along(array, dim, size):
    before, after = (array.shape[:dim], array.shape[dim + 1 :])
    return jnp.moveaxis(array.reshape(*before, size, -1, *after), dim, 0)


def summed_on_arrival(array, axis, dim):
    pieces = cut_along(array, dim, lax.axis_size(axis))
    arrived = lax.all_to_all(pieces, axis, split_axis=0, concat_axis=0, tiled=True)
    return arrived.sum(axis=0)


def join_stats(first, second):
    highest = jnp.maximum(first[0], second[0])
    summed = first[1] * jnp.exp(first[0] - highest) + second[1] * jnp.exp(second[0] - highest)
    return (highest, summed)


def shards(tokens, slot_keys, expert_in, expert_out):
    images, positions, features = tokens.shape
    own_slots = slot_keys.shape[1]
    experts = expert_in.shape[0]
    per_expert = own_slots // experts
    all_keys = lax.all_gather(slot_keys, SLOT, axis=1, tiled=True)
    flat = tokens.reshape(images * positions, features)
    logits = jnp.dot(flat, all_keys, preferred_element_type=jnp.float32).reshape(
        images, positions, -1
    )
    local_peak = jnp.max(logits, axis=1)
    local_sum = jnp.sum(jnp.exp(logits - local_peak[:, None, :]), axis=1)
    peak, totals = merged((local_peak, local_sum), SLOT, join_stats)
    raised = jnp.exp(logits - peak[:, None, :])
    first_slot = lax.axis_index(SLOT) * own_slots
    own_totals = lax.dynamic_slice_in_dim(totals, first_slot, own_slots, 1)
    weights = raised.astype(jnp.bfloat16)
    summed = summed_rows(
        jnp.einsum("bms,bmd->sbd", weights, tokens, preferred_element_type=jnp.float32), SLOT
    )
    slot_inputs = (summed / own_totals.T[:, :, None]).astype(jnp.bfloat16)
    everyone = gathered_copies(slot_inputs, "dp", 1)
    length = images * lax.axis_size("dp")
    expert_rows = everyone.reshape(experts, per_expert * length, features)
    hidden = jnp.einsum("erd,edf->erf", expert_rows, expert_in, preferred_element_type=jnp.float32)
    hidden = jax.nn.gelu(hidden, approximate=True).astype(jnp.bfloat16)
    result = jnp.einsum("erf,efd->erd", hidden, expert_out, preferred_element_type=jnp.float32)
    slot_results = summed_on_arrival(
        jnp.transpose(result.reshape(own_slots, length, features), (1, 0, 2)), "dp", 0
    ).astype(jnp.bfloat16)
    mix = jax.nn.softmax(logits, axis=2).astype(jnp.bfloat16)
    combined = jnp.einsum(
        "bms,bsd->bmd",
        mix,
        lax.all_gather(slot_results, SLOT, axis=1, tiled=True),
        preferred_element_type=jnp.float32,
    )
    return combined.astype(jnp.bfloat16)


def solution(mesh):
    split = Mesh(
        mesh.devices.reshape(4, 4, 2, mesh.shape["dp"]), ("slot_0", "slot_1", "slot_2", "dp")
    )
    return jax.shard_map(
        shards,
        mesh=split,
        in_specs=(P("dp", SLOT, None), P(None, SLOT), P(SLOT, None, "dp"), P(SLOT, "dp", None)),
        out_specs=P("dp", SLOT, None),
        check_vma=False,
    )
```

profile of v0, /device:TPU:0, one launch (start us, length us, event | category | flops | bytes accessed | tf_op | source)
XLA Modules:
  0.0 450.6 jit_solution(11117423069919956325)
XLA Ops:
  6.5 0.7 all-gather.3.cloned.1.call-update
  7.3 0.0 reduce-scatter.4.cloned.1.call-start
  7.3 76.1 %all-gather.3.cloned.1.call-done = bf16[1024,1024]{0,1:T(8,128)(2,1)} async-done(((bf16[1024,32]{0,1:T(8,128)(2,1)}), bf16[1024,1024]{0,1:T(8,128)(2,1)}) %all-gather.3.cloned.1.call-update) | async-done | bytes 2097168 | tf_op jit(solution)/shard_map/all_gather | solution.py:84
  83.4 2.6 fusion.33
  86.0 0.2 exponential_reduce_fusion
  86.3 0.1 broadcast_in_dim.4
  86.4 21.6 %all_to_all.15 = f32[32,6,1024]{2,1,0:T(8,128)S(1)} all-to-all(f32[32,6,1024]{2,1,0:T(8,128)S(1)} %broadcast_in_dim.4), channel_id=1, replica_groups=mesh['slot_0'=4,'slot_1'=4,'slot_2'=2,'dp'=4] {'slot_0','slot_1','slot_2'}, dimensions={0} | all-to-all | bytes 1572864 | tf_op jit(solution)/shard_map/all_to_all | solution.py:12
  108.1 0.3 fusion.30
  108.4 0.2 multiply_add_fusion
  108.6 0.1 multiply_add_fusion.1
  108.7 0.1 multiply_add_fusion.2
  108.8 6.4 %convolution_bitcast_fusion = f32[1024,3,1024]{2,0,1:T(8,128)} fusion(bf16[3,128,1024]{2,1,0:T(8,128)(2,1)S(1)} %copy-done, f32[3,128,1024]{2,1,0:T(8,128)S(1)} %get-tuple-element.21, f32[3,1024]{1,0:T(4,128)S(1)} %bitcast.26), kind=kOutput, calls=%fused_computation.1 | convolution fusion | flops 806092800 | bytes 14954496 | tf_op jit(solution)/shard_map/bms,bmd->sbd/dot_general | solution.py:97
  115.3 0.0 reduce-scatter.6.cloned.1.call-start
  115.3 110.5 %reduce-scatter.4.cloned.1.call-done = f32[256,3,1024]{2,0,1:T(8,128)} async-done(((f32[1024,3,1024]{2,0,1:T(8,128)}), f32[256,3,1024]{2,0,1:T(8,128)}) %reduce-scatter.4.cloned.1.call-update) | async-done | bytes 3145744 | tf_op jit(solution)/shard_map/reduce_scatter | solution.py:47
  225.8 0.0 reduce-scatter.8.cloned.1.call-start
  225.9 40.6 %reduce-scatter.6.cloned.1.call-done = f32[64,3,1024]{2,0,1:T(8,128)} async-done(((f32[256,3,1024]{2,0,1:T(8,128)}), f32[64,3,1024]{2,0,1:T(8,128)}) %reduce-scatter.6.cloned.1.call-update) | async-done | bytes 786448 | tf_op jit(solution)/shard_map/reduce_scatter | solution.py:47
  266.5 0.0 all-gather.5.cloned.1.call-start
  266.5 0.1 fusion.22
  266.6 23.2 %reduce-scatter.8.cloned.1.call-done = f32[32,3,1024]{2,0,1:T(8,128)} async-done(((f32[64,3,1024]{2,0,1:T(8,128)}), f32[32,3,1024]{2,0,1:T(8,128)}) %reduce-scatter.8.cloned.1.call-update) | async-done | bytes 393232 | tf_op jit(solution)/shard_map/reduce_scatter | solution.py:47
  289.9 1.1 divide_convert_fusion.2
  290.9 0.1 broadcast_in_dim.5
  291.0 14.0 %all_to_all.16 = bf16[4,32,3,1024]{3,1,2,0:T(8,128)(2,1)S(1)} all-to-all(bf16[4,32,3,1024]{3,1,2,0:T(8,128)(2,1)S(1)} %broadcast_in_dim.5), channel_id=1, replica_groups=mesh['slot_0'=4,'slot_1'=4,'slot_2'=2,'dp'=4] {'dp'}, dimensions={0} | all-to-all | bytes 1572864 | tf_op jit(solution)/shard_map/all_to_all | solution.py:12
  305.1 0.7 copy.11
  305.8 1.4 reshape_reshape.3
  307.2 10.0 %fusion.13 = f32[4,96,1024]{2,1,0:T(8,128)} fusion(bf16[4,1024,1024]{2,1,0:T(8,128)(2,1)} %param.7, bf16[4,96,1024]{2,1,0:T(8,128)(2,1)} %reshape_reshape.3, bf16[4,1024,1024]{2,1,0:T(8,128)(2,1)} %param.6), kind=kOutput, calls=%fused_computation.19 | convolution fusion | flops 1614151680 | bytes 19136512 | tf_op jit(solution)/shard_map/erf,efd->erd/dot_general | solution.py:105
  317.2 2.7 reshape.20
  319.9 2.5 copy.12
  322.4 23.2 %all_to_all.17 = f32[4,3,32,1024]{3,2,1,0:T(8,128)} all-to-all(f32[4,3,32,1024]{3,2,1,0:T(8,128)S(1)} %bitcast.24), channel_id=1, replica_groups=mesh['slot_0'=4,'slot_1'=4,'slot_2'=2,'dp'=4] {'dp'}, dimensions={0} | all-to-all | bytes 3145728 | tf_op jit(solution)/shard_map/all_to_all | solution.py:69
  345.6 2.2 reduce_sum.29
  347.9 0.4 fusion.34
  348.3 90.9 %all-gather.5.cloned.1.call-done = bf16[3,1024,1024]{2,1,0:T(8,128)(2,1)} async-done(((bf16[3,32,1024]{2,1,0:T(8,128)(2,1)}), bf16[3,1024,1024]{2,1,0:T(8,128)(2,1)}) %all-gather.5.cloned.1.call-update) | async-done | bytes 6291472 | tf_op jit(solution)/shard_map/all_gather | solution.py:113
  439.1 4.9 %convolution_convert_fusion = bf16[3,128,1024]{2,1,0:T(8,128)(2,1)} fusion(bf16[3,1024,1024]{2,1,0:T(8,128)(2,1)} %all-gather.5.cloned.1.call-done, f32[3,128]{1,0:T(4,128)S(1)} %fusion.34, f32[3,128,1024]{2,1,0:T(8,128)S(1)} %get-tuple-element.21), kind=kOutput, calls=%fused_computation.18 | convolution fusion | flops 806880640 | bytes 8652288 | tf_op jit(solution)/shard_map/bms,bsd->bmd/dot_general | solution.py:110
  (10 shorter events, 0.1 us)
Async XLA Ops:
  6.5 76.9 %copy-start = (bf16[3,128,1024]{2,1,0:T(8,128)(2,1)S(1)}, bf16[3,128,1024]{2,1,0:T(8,128)(2,1)}, u32[]{:S(2)}) copy-start(bf16[3,128,1024]{2,1,0:T(8,128)(2,1)} %param.4) | copy-start | bytes 2359300
  6.5 76.9 %all-gather.3.cloned.1.call-start = ((), (), s32[]{:S(2)}) async-start(), calls=%async_computation.6 | async-start | bytes 2162688 | tf_op jit(solution)/shard_map/all_gather | solution.py:84
  7.3 218.5 %reduce-scatter.4.cloned.1.call-start = ((), (), s32[]{:S(2)}) async-start(), calls=%async_computation.7 | async-start | bytes 15728640 | tf_op jit(solution)/shard_map/reduce_scatter | solution.py:47
  115.3 151.2 %reduce-scatter.6.cloned.1.call-start = ((), (), s32[]{:S(2)}) async-start(), calls=%async_computation.8 | async-start | bytes 3932160 | tf_op jit(solution)/shard_map/reduce_scatter | solution.py:47
  225.8 64.0 %reduce-scatter.8.cloned.1.call-start = ((), (), s32[]{:S(2)}) async-start(), calls=%async_computation.9 | async-start | bytes 1179648 | tf_op jit(solution)/shard_map/reduce_scatter | solution.py:47
  266.5 172.7 %all-gather.5.cloned.1.call-start = ((), (), s32[]{:S(2)}) async-start(), calls=%async_computation.10 | async-start | bytes 6488064 | tf_op jit(solution)/shard_map/all_gather | solution.py:113
Sparse Core Ops, SparseCore 0:
  10.3 73.0 all-gather.2
  115.4 110.3 reduce-scatter.3
  228.2 38.2 reduce-scatter.5
  268.7 21.1 reduce-scatter.7
  348.0 91.1 all-gather.4
where the time goes:
time: 451 us
  waiting for transfers between devices  342 us (76%)
  blocking collectives  58.9 us (13%)
  matrix products  24 us (5%)
  between operations  13.2 us (3%)
  local copies, waits for them, and re-layouts  7.76 us (2%)
    reduce_scatter x3, waiting for transfers between devices, summed_rows(): total = lax.psum_scatter(total, axis, scatter_dimension=0, tiled=True)  174 us
    all_gather x1, waiting for transfers between devices, shards(): lax.all_gather(slot_results, SLOT, axis=1, tiled=True)  90.9 us
    all_gather x1, waiting for transfers between devices, shards(): all_keys = lax.all_gather(slot_keys, SLOT, axis=1, tiled=True)  76.1 us
    all_to_all x2, blocking collectives, from_everyone(): return lax.all_to_all(copies, axis, split_axis=0, concat_axis=0, tiled=True)  35.7 us
    all_to_all x1, blocking collectives, summed_on_arrival(): lax.all_to_all(pieces, axis, split_axis=0, concat_axis=0, tiled=True)  23.2 us
    dot_general x1, matrix products, shards(): jnp.einsum('erf,efd->erd', hidden, expert_out, preferred_element_type=jnp...  10 us
  transfers between devices with their start and end apart: 5, of which 5 were waited for; matrix products, arithmetic and copies ran while one was open for 0% of the time, Pallas kernels for 0%

commit v1 on v0

--- a/solution.py
+++ b/solution.py
@@ -1,3 +1,4 @@
+import functools
 import jax
 import jax.numpy as jnp
 from jax import lax
@@ -5,6 +6,15 @@
 from jax.sharding import PartitionSpec as P
 
 SLOT = ("slot_0", "slot_1", "slot_2")
+
+
+def set_spans(xx, which_axis, pos_dim):
+    return jnp.concatenate(
+        lax.all_to_all(jnp.stack([xx] * lax.axis_size(which_axis)), which_axis, 0, 0), axis=pos_dim
+    )
+
+
+step_on_loads = functools.partial(set_spans, which_axis=SLOT, pos_dim=1)
 
 
 def from_everyone(array, axis):
@@ -81,7 +91,7 @@
     own_slots = slot_keys.shape[1]
     experts = expert_in.shape[0]
     per_expert = own_slots // experts
-    all_keys = lax.all_gather(slot_keys, SLOT, axis=1, tiled=True)
+    all_keys = step_on_loads(slot_keys)
     flat = tokens.reshape(images * positions, features)
     logits = jnp.dot(flat, all_keys, preferred_element_type=jnp.float32).reshape(
         images, positions, -1

time: 451 us -> 416 us (0.922)
  waiting for transfers between devices: 342 us -> 265 us
  blocking collectives: 58.9 us -> 101 us
    all_gather x1 -> x0, waiting for transfers between devices: 76.1 us -> none  [shards(): all_keys = lax.all_gather(slot_keys, SLOT, axis=1, tiled=True)]
    all_to_all x0 -> x1, blocking collectives: none -> 40.9 us  [set_spans(): lax.all_to_all(jnp.stack([xx] * lax.axis_size(which_axis)), which_axis, 0...]
  transfers between devices with their start and end apart: 5 -> 4, of which waited for: 5 -> 4; matrix products, arithmetic and copies ran while one was open for 0% -> 0% of each run, Pallas kernels for 0% -> 0%
where the time goes in v1:
time: 416 us
  waiting for transfers between devices  265 us (64%)
  blocking collectives  101 us (24%)
  matrix products  22.4 us (5%)
  between operations  13.2 us (3%)
  local copies, waits for them, and re-layouts  8.92 us (2%)
  other arithmetic  4.48 us (1%)
    reduce_scatter x3, waiting for transfers between devices, summed_rows(): total = lax.psum_scatter(total, axis, scatter_dimension=0, tiled=True)  174 us
    all_gather x1, waiting for transfers between devices, shards(): lax.all_gather(slot_results, SLOT, axis=1, tiled=True)  90.9 us
    all_to_all x1, blocking collectives, set_spans(): lax.all_to_all(jnp.stack([xx] * lax.axis_size(which_axis)), which_axis, 0...  40.9 us
    all_to_all x2, blocking collectives, from_everyone(): return lax.all_to_all(copies, axis, split_axis=0, concat_axis=0, tiled=True)  36.9 us
    all_to_all x1, blocking collectives, summed_on_arrival(): lax.all_to_all(pieces, axis, split_axis=0, concat_axis=0, tiled=True)  23.2 us
    dot_general x1, matrix products, shards(): jnp.einsum('erf,efd->erd', hidden, expert_out, preferred_element_type=jnp...  10 us
  transfers between devices with their start and end apart: 4, of which 4 were waited for; matrix products, arithmetic and copies ran while one was open for 0% of the time, Pallas kernels for 0%

profile of v1, /device:TPU:0, one launch (start us, length us, event | category | flops | bytes accessed | tf_op | source)
XLA Modules:
  0.0 415.5 jit_solution(696105563767812728)
XLA Ops:
  6.5 1.2 stack.2
  7.7 40.9 %all_to_all.20 = bf16[32,1024,32]{1,2,0:T(8,128)(2,1)S(1)} all-to-all(bf16[32,1024,32]{1,2,0:T(8,128)(2,1)S(1)} %stack.2), channel_id=1, replica_groups=mesh['slot_0'=4,'slot_1'=4,'slot_2'=2,'dp'=4] {'slot_0','slot_1','slot_2'}, dimensions={0} | all-to-all | bytes 4194304 | tf_op jit(solution)/shard_map/all_to_all | solution.py:13
  48.6 1.1 fusion.31
  49.7 0.2 exponential_reduce_fusion
  50.0 0.1 broadcast_in_dim.4
  50.1 22.8 %all_to_all.21 = f32[32,6,1024]{2,1,0:T(8,128)S(1)} all-to-all(f32[32,6,1024]{2,1,0:T(8,128)S(1)} %broadcast_in_dim.4), channel_id=1, replica_groups=mesh['slot_0'=4,'slot_1'=4,'slot_2'=2,'dp'=4] {'slot_0','slot_1','slot_2'}, dimensions={0} | all-to-all | bytes 1572864 | tf_op jit(solution)/shard_map/all_to_all | solution.py:22
  72.9 0.3 fusion.28
  73.2 0.2 multiply_add_fusion
  73.4 0.1 multiply_add_fusion.1
  73.5 0.1 multiply_add_fusion.2
  73.7 6.4 %convolution_bitcast_fusion = f32[1024,3,1024]{2,0,1:T(8,128)} fusion(bf16[3,128,1024]{2,1,0:T(8,128)(2,1)S(1)} %copy-done, f32[3,128,1024]{2,1,0:T(8,128)S(1)} %get-tuple-element.21, f32[3,1024]{1,0:T(4,128)S(1)} %bitcast.28), kind=kOutput, calls=%fused_computation.1 | convolution fusion | flops 806092800 | bytes 14954496 | tf_op jit(solution)/shard_map/bms,bmd->sbd/dot_general | solution.py:107
  80.1 0.0 reduce-scatter.4.cloned.1.call-update
  80.1 0.0 reduce-scatter.6.cloned.1.call-start
  80.2 110.4 %reduce-scatter.4.cloned.1.call-done = f32[256,3,1024]{2,0,1:T(8,128)} async-done(((f32[1024,3,1024]{2,0,1:T(8,128)}), f32[256,3,1024]{2,0,1:T(8,128)}) %reduce-scatter.4.cloned.1.call-update) | async-done | bytes 3145744 | tf_op jit(solution)/shard_map/reduce_scatter | solution.py:57
  190.6 0.0 reduce-scatter.8.cloned.1.call-start
  190.6 40.6 %reduce-scatter.6.cloned.1.call-done = f32[64,3,1024]{2,0,1:T(8,128)} async-done(((f32[256,3,1024]{2,0,1:T(8,128)}), f32[64,3,1024]{2,0,1:T(8,128)}) %reduce-scatter.6.cloned.1.call-update) | async-done | bytes 786448 | tf_op jit(solution)/shard_map/reduce_scatter | solution.py:57
  231.3 0.0 all-gather.2.cloned.1.call-start
  231.3 0.1 fusion.20
  231.4 23.4 %reduce-scatter.8.cloned.1.call-done = f32[32,3,1024]{2,0,1:T(8,128)} async-done(((f32[64,3,1024]{2,0,1:T(8,128)}), f32[32,3,1024]{2,0,1:T(8,128)}) %reduce-scatter.8.cloned.1.call-update) | async-done | bytes 393232 | tf_op jit(solution)/shard_map/reduce_scatter | solution.py:57
  254.8 1.1 divide_convert_fusion.2
  255.9 0.1 broadcast_in_dim.5
  256.0 14.0 %all_to_all.22 = bf16[4,32,3,1024]{3,1,2,0:T(8,128)(2,1)S(1)} all-to-all(bf16[4,32,3,1024]{3,1,2,0:T(8,128)(2,1)S(1)} %broadcast_in_dim.5), channel_id=1, replica_groups=mesh['slot_0'=4,'slot_1'=4,'slot_2'=2,'dp'=4] {'dp'}, dimensions={0} | all-to-all | bytes 1572864 | tf_op jit(solution)/shard_map/all_to_all | solution.py:22
  270.0 0.7 copy.14
  270.7 1.4 reshape_reshape.3
  272.1 10.0 %fusion.11 = f32[4,96,1024]{2,1,0:T(8,128)} fusion(bf16[4,1024,1024]{2,1,0:T(8,128)(2,1)} %param.7, bf16[4,96,1024]{2,1,0:T(8,128)(2,1)} %reshape_reshape.3, bf16[4,1024,1024]{2,1,0:T(8,128)(2,1)} %param.6), kind=kOutput, calls=%fused_computation.17 | convolution fusion | flops 1614151680 | bytes 19136512 | tf_op jit(solution)/shard_map/erf,efd->erd/dot_general | solution.py:115
  282.2 2.7 reshape.30
  284.8 2.5 copy.15
  287.3 23.2 %all_to_all.23 = f32[4,3,32,1024]{3,2,1,0:T(8,128)} all-to-all(f32[4,3,32,1024]{3,2,1,0:T(8,128)S(1)} %bitcast.25), channel_id=1, replica_groups=mesh['slot_0'=4,'slot_1'=4,'slot_2'=2,'dp'=4] {'dp'}, dimensions={0} | all-to-all | bytes 3145728 | tf_op jit(solution)/shard_map/all_to_all | solution.py:79
  310.6 2.2 reduce_sum.29
  312.8 0.4 fusion.32
  313.2 90.9 %all-gather.2.cloned.1.call-done = bf16[3,1024,1024]{2,1,0:T(8,128)(2,1)} async-done(((bf16[3,32,1024]{2,1,0:T(8,128)(2,1)}), bf16[3,1024,1024]{2,1,0:T(8,128)(2,1)}) %all-gather.2.cloned.1.call-update) | async-done | bytes 6291472 | tf_op jit(solution)/shard_map/all_gather | solution.py:123
  404.1 4.9 %convolution_convert_fusion = bf16[3,128,1024]{2,1,0:T(8,128)(2,1)} fusion(bf16[3,1024,1024]{2,1,0:T(8,128)(2,1)} %all-gather.2.cloned.1.call-done, f32[3,128]{1,0:T(4,128)S(1)} %fusion.32, f32[3,128,1024]{2,1,0:T(8,128)S(1)} %get-tuple-element.21), kind=kOutput, calls=%fused_computation.16 | convolution fusion | flops 806880640 | bytes 8652288 | tf_op jit(solution)/shard_map/bms,bsd->bmd/dot_general | solution.py:120
  (9 shorter events, 0.1 us)
Async XLA Ops:
  6.5 42.1 %copy-start = (bf16[3,128,1024]{2,1,0:T(8,128)(2,1)S(1)}, bf16[3,128,1024]{2,1,0:T(8,128)(2,1)}, u32[]{:S(2)}) copy-start(bf16[3,128,1024]{2,1,0:T(8,128)(2,1)} %param.4) | copy-start | bytes 2359300
  6.5 184.0 %reduce-scatter.4.cloned.1.call-start = ((), (), s32[]{:S(2)}) async-start(), calls=%async_computation.7 | async-start | bytes 15728640 | tf_op jit(solution)/shard_map/reduce_scatter | solution.py:57
  80.1 151.2 %reduce-scatter.6.cloned.1.call-start = ((), (), s32[]{:S(2)}) async-start(), calls=%async_computation.8 | async-start | bytes 3932160 | tf_op jit(solution)/shard_map/reduce_scatter | solution.py:57
  190.6 64.2 %reduce-scatter.8.cloned.1.call-start = ((), (), s32[]{:S(2)}) async-start(), calls=%async_computation.9 | async-start | bytes 1179648 | tf_op jit(solution)/shard_map/reduce_scatter | solution.py:57
  231.3 172.8 %all-gather.2.cloned.1.call-start = ((), (), s32[]{:S(2)}) async-start(), calls=%async_computation.10 | async-start | bytes 6488064 | tf_op jit(solution)/shard_map/all_gather | solution.py:123
Sparse Core Ops, SparseCore 0:
  80.2 110.3 reduce-scatter.3
  193.0 38.2 reduce-scatter.5
  233.6 21.1 reduce-scatter.7
  312.9 91.1 all-gather.1
